TPU v7x, 32 devices: a whole 2x2x4 slice. The times are simulated.
32 devices in a mesh: member: 2 (over y), blk: 16 (over z, x, core).
Axes of the slice: x: 2, y: 2, z: 4, core: 2. Of those that a mesh axis runs over, the one named last changes fastest.
Arguments:
- pressure: float32 [55, 8192], P(None, ('member', 'blk')), parts along dimension 1, may hold values from -6 to 6
- velocity: float32 [55, 24576], P(None, ('member', 'blk')), parts along dimension 1, may hold values from -3 to 3
- tracers: float32 [3, 55, 8192], P(None, None, ('member', 'blk')), parts along dimension 2, may hold values from 0.1 to 2
- tendency: float32 [55, 8192], P(None, ('member', 'blk')), parts along dimension 1, may hold values from -6 to 6
- pattern: float32 [8192], P(('member', 'blk')), parts along dimension 0, may hold values from -0.9 to 0.9
- coupling: float32 [55, 4096], P(None, 'blk'), may hold values from 0.3 to 3
- edge_length: float32 [12288], P('blk'), may hold values from 0.7 to 1.4
- inv_distance: float32 [12288], P('blk'), may hold values from 0.7 to 1.4
- inv_area: float32 [4096], P('blk'), may hold values from 0.7 to 1.4
- edge_ends: int32 [2, 12288], P(None, 'blk'), may hold values from 0 to 351, as said below
- halo_ends: int32 [2, 2048], P(None, 'blk'), may hold values from 0 to 351, as said below
- cell_edges: int32 [8, 4096], P(None, 'blk'), may hold values from 0 to 895, as said below
- cell_signs: int32 [8, 4096], P(None, 'blk'), may hold values from -1 to 1, as said below
- cell_send: int32 [6, 256], P(None, 'blk'), may hold values from 0 to 255, as said below
- edge_send: int32 [4, 512], P(None, 'blk'), may hold values from 0 to 767, as said below
Outputs:
- new_pressure: float32 [55, 8192], P(None, ('member', 'blk')), parts along dimension 1
- new_velocity: float32 [55, 24576], P(None, ('member', 'blk')), parts along dimension 1
- new_tracers: float32 [3, 55, 8192], P(None, None, ('member', 'blk')), parts along dimension 2
There are 2 independent parts, one for each index of `member`. A program takes and returns all parts, laid end to end along the dimension named above; an argument that names none is the same for every part. Nothing has to cross between parts.
Inputs may be any that keep to these rules, and one draw needn't show every extreme that they name: `cell_send`: the cells form a periodic hexagonal lattice; each device holds a 16 x 16 patch, numbered in a drawn order; a patch touches the patches of the devices at index offsets 1, -1, 4, -4, 3 and 1 - 4 (modulo 16). Row k of a device's block lists the own cells that the device at index + o_k receives, o = (1, -1, 4, -4, 3, 1 - 4); rows 0 to 3 hold 16 live entries, rows 4 and 5 one live entry first, the rest repeat it. `edge_send`: row k of a device's block lists the own edges that the device at index + p_k receives, p = (1, 4, -4, 1 - 4); the live entries come first, 31, 16, 15 and 1 of them, the rest repeat a live one. `edge_ends`: row 0 is an own cell; row 1 is the neighbouring cell, own or received; the numbering is consistent with cell_send. `halo_ends`: for live received slots, the owner's edge's start and end as the receiver numbers them; other slots hold cells that no output reads. `cell_edges`: each own cell lists its six edges once each, in a drawn order, and two unused entries, whose sign is 0. `cell_signs`: 1 where the cell is the edge's start, -1 where it is its end, 0 on the unused entries.
All inputs are finite; a program needn't handle non-finite values.
Results may differ from a plain program's by a relative error of at most 0.0003.
Values sent between devices are 32-bit elements; how exact they have to be, the bound alone decides.
A program may use at most 128 MiB of HBM per device.

v0:
```python
import functools

import jax
import jax.numpy as jnp
from jax import lax
from jax.experimental import pallas as pl
from jax.experimental.pallas import tpu as pltpu
from jax.sharding import PartitionSpec as P

SUBSTEPS = 6
grad_scale = 0.25
spread_scale = 0.25
force_scale = 0.5
tracer_scale = 0.05

F32 = jnp.float32
BF16 = jnp.bfloat16
MESH = pl.DeviceIdType.MESH
LANES = 128


def up_to(value, unit):
    return -(-value // unit) * unit


def dot(a, b):
    return jnp.dot(a, b, preferred_element_type=F32)


def halves(x):
    high = x.astype(BF16).astype(F32)
    return jnp.concatenate([high, x - high], axis=0).astype(BF16)


def fold(x):
    rows = x.shape[0] // 2
    return x[:rows] + x[rows:]


def pick(x, table):
    return fold(dot(halves(x), table))


def pad_rows(x, rows):
    if x.shape[0] == rows:
        return x
    return jnp.concatenate([x, jnp.zeros((rows - x.shape[0], x.shape[1]), x.dtype)], axis=0)


def pad_lanes(x, lanes, value=0):
    if x.shape[1] == lanes:
        return x
    return jnp.concatenate(
        [x, jnp.full((x.shape[0], lanes - x.shape[1]), value, x.dtype)], axis=1
    )


def one_hot(rows, index):
    where = lax.broadcasted_iota(jnp.int32, (rows, index.shape[1]), 0)
    return jnp.where(where == index, 1.0, 0.0)


def down(x, steps, fill=None):
    moved = pltpu.roll(x, steps, 0)
    if fill is None:
        return moved
    rows = lax.broadcasted_iota(jnp.int32, x.shape, 0)
    return jnp.where(rows < steps, fill, moved)


def up(x, steps, fill=None):
    moved = pltpu.roll(x, x.shape[0] - steps, 0)
    if fill is None:
        return moved
    rows = lax.broadcasted_iota(jnp.int32, x.shape, 0)
    return jnp.where(rows >= x.shape[0] - steps, fill, moved)


def strides(rows):
    found = []
    step = 1
    while step < rows:
        found.append(step)
        step *= 2
    return found


def factor_columns(c, levels, inv_ref, a_ref, b_ref):
    rows = c.shape[0]
    above = up(c, 1, 0.0)
    m = [1.0 + c, c, jnp.ones_like(c), c]
    for step in strides(rows):
        if step >= 16:
            scale = 1.0 / (m[0] + m[1] + m[2] + m[3])
            m = [entry * scale for entry in m]
        o = [
            down(m[0], step, 1.0),
            down(m[1], step, 0.0),
            down(m[2], step, 0.0),
            down(m[3], step, 1.0),
        ]
        m = [
            m[0] * o[0] + m[1] * o[2],
            m[0] * o[1] + m[1] * o[3],
            m[2] * o[0] + m[3] * o[2],
            m[2] * o[1] + m[3] * o[3],
        ]
    inverse = 1.0 / (above + m[0] / m[2])
    inv_ref[...] = inverse
    row = lax.broadcasted_iota(jnp.int32, c.shape, 0)
    a = jnp.where(row < 1, 0.0, c * inverse)
    b = jnp.where(row >= levels - 1, 0.0, above * inverse)
    for number, step in enumerate(strides(rows)):
        a_ref[number] = a
        b_ref[number] = b
        a = a * down(a, step, 0.0)
        b = b * up(b, step, 0.0)


def solve(source, lanes, inv_ref, a_ref, b_ref):
    y = source * inv_ref[:, lanes]
    steps = strides(source.shape[0])
    for number, step in enumerate(steps):
        y = y + a_ref[number, :, lanes] * down(y, step)
    for number, step in enumerate(steps):
        y = y + b_ref[number, :, lanes] * up(y, step)
    return y


def kernel(
    cell_offsets, edge_offsets,
    p_ref, u_ref, t_ref, tend_ref, pat_ref, coup_ref, len_ref, dist_ref, area_ref,
    ends_ref, hends_ref, ce_ref, cs_ref, csend_ref, esend_ref,
    p_out, u_out, t_out,
    send0, recv0, esend, erecv, sends, recvs,
    gs_ref, ge_ref, gc_ref, d_ref, wh_ref, wl_ref, a_ref, b_ref, inv_ref, trs_ref, tre_ref,
    send0_sem, recv0_sem, esend_sem, erecv_sem, sends_sem, recvs_sem,
):
    count = lax.axis_size("blk")
    member = lax.axis_index("member")
    me = lax.axis_index("blk")

    def peer(offset):
        return (member, lax.rem(me + (offset + count), count))

    barrier = pltpu.get_barrier_semaphore()
    for offset in cell_offsets:
        pl.semaphore_signal(barrier, inc=1, device_id=peer(offset), device_id_type=MESH)

    levels, own = p_ref.shape
    species = t_ref.shape[0]
    owned = u_ref.shape[1]
    peers, slots = csend_ref.shape
    epeers, eslots = esend_ref.shape
    rows = up_to(levels, 8)
    rim = up_to(peers * slots, LANES)
    hal = peers * slots
    ehal = epeers * eslots
    OWN = slice(0, own)
    RIM = slice(own, own + rim)

    csend = jnp.concatenate([csend_ref[k : k + 1, :] for k in range(peers)], axis=1)
    sel = one_hot(own, pad_lanes(csend, rim, -1)).astype(BF16)
    esel_row = jnp.concatenate([esend_ref[k : k + 1, :] for k in range(epeers)], axis=1)
    esel = one_hot(owned, esel_row).astype(BF16)

    pressure = pad_rows(p_ref[...], rows)
    tracers = [pad_rows(t_ref[s], rows) for s in range(species)]
    coupling = pad_rows(coup_ref[...], rows)
    height = lax.broadcasted_iota(jnp.int32, (levels, own), 0).astype(F32)
    taper = jnp.minimum(1.0, (levels - 1.0 - height) / (0.25 * levels))
    forcing = pad_rows(force_scale * (1.0 + pat_ref[...] * taper) * tend_ref[...], rows)
    area = area_ref[...]
    area8 = pad_rows(area, 8)
    sent = pick(jnp.concatenate([pressure] + tracers, axis=0), sel)
    wide = send0.shape[1]
    send0[...] = jnp.transpose(pad_rows(sent, wide))[:hal]
    edges = jnp.concatenate(
        [pad_rows(u_ref[...], rows), len_ref[...], dist_ref[...], jnp.zeros((6, owned), F32)],
        axis=0,
    )
    esend[...] = jnp.transpose(pad_rows(pick(edges, esel), LANES))

    pl.semaphore_wait(barrier, len(cell_offsets))
    first = []
    for k, offset in enumerate(cell_offsets):
        copy = pltpu.make_async_remote_copy(
            src_ref=send0.at[pl.ds(k * slots, slots)],
            dst_ref=recv0.at[pl.ds(k * slots, slots)],
            send_sem=send0_sem.at[k],
            recv_sem=recv0_sem.at[k],
            device_id=peer(offset),
            device_id_type=MESH,
        )
        copy.start()
        first.append(copy)
    efirst = []
    for k, offset in enumerate(edge_offsets):
        copy = pltpu.make_async_remote_copy(
            src_ref=esend.at[pl.ds(k * eslots, eslots)],
            dst_ref=erecv.at[pl.ds(k * eslots, eslots)],
            send_sem=esend_sem.at[k],
            recv_sem=erecv_sem.at[k],
            device_id=peer(offset),
            device_id_type=MESH,
        )
        copy.start()
        efirst.append(copy)

    column = jnp.concatenate([coupling, forcing, area8], axis=0)
    column_rim = pick(column, sel)
    force_own, force_rim = forcing, column_rim[rows : 2 * rows]
    area_rim = column_rim[2 * rows : 2 * rows + 1]
    area_all = jnp.concatenate([area, area_rim], axis=1)
    factor_columns(
        jnp.concatenate([coupling, column_rim[:rows]], axis=1), levels, inv_ref, a_ref, b_ref
    )

    start = jnp.concatenate([ends_ref[0:1, :], hends_ref[0:1, :]], axis=1)
    end = jnp.concatenate([ends_ref[1:2, :], hends_ref[1:2, :]], axis=1)
    ext = own + rim
    gs_ref[...] = one_hot(ext, start).astype(BF16)
    ge_ref[...] = one_hot(ext, end).astype(BF16)
    total = owned + ehal
    where = lax.broadcasted_iota(jnp.int32, (total, own), 0)
    table = jnp.zeros((total, own), F32)
    for j in range(ce_ref.shape[0]):
        sign = cs_ref[j : j + 1, :]
        index = jnp.where(sign == 0, -1, ce_ref[j : j + 1, :])
        table = jnp.where(where == index, sign.astype(F32), table)
    d_ref[:, OWN] = table.astype(BF16)
    d_ref[:, RIM] = dot(d_ref[:, OWN], sel).astype(BF16)

    for copy in efirst:
        copy.wait_recv()
    edges = jnp.concatenate([edges, jnp.transpose(erecv[...])[: edges.shape[0]]], axis=1)
    velocity = edges[:rows]
    length = edges[rows : rows + 1]
    distance = edges[rows + 1 : rows + 2]
    conduct = (spread_scale * grad_scale) * length * distance
    conduct_high = conduct.astype(BF16).astype(F32)
    gd = ge_ref[...].astype(F32) - gs_ref[...].astype(F32)
    gc_ref[:ext] = (gd * conduct_high).astype(BF16)
    gc_ref[ext:] = (gd * (conduct - conduct_high)).astype(BF16)
    weight = fold(dot(gc_ref[...], d_ref[...])) * area_all
    weight_high = weight.astype(BF16)
    wh_ref[...] = weight_high
    wl_ref[...] = (weight - weight_high.astype(F32)).astype(BF16)
    spread = pick(velocity * length, d_ref[...]) * (spread_scale * area_all)
    q_own, q_rim = spread[:, OWN], spread[:, RIM]

    for copy in first:
        copy.wait_recv()
    arrived = jnp.transpose(pad_rows(recv0[...], rim))
    halo = arrived[:rows]
    tracer_ext = jnp.concatenate(
        [
            jnp.concatenate([tracers[s], arrived[(s + 1) * rows : (s + 2) * rows]], axis=1)
            for s in range(species)
        ],
        axis=0,
    )

    def through(x, rows_of, lanes):
        parts = halves(x)
        return fold(dot(parts, wh_ref[rows_of, lanes])) + dot(
            parts[: x.shape[0]], wl_ref[rows_of, lanes]
        )

    p_own, p_rim = pressure, sent[:rows]
    sum_one = jnp.zeros((rows, ext), F32)
    sum_two = jnp.zeros((rows, ext), F32)
    lap_own = through(p_own, OWN, slice(0, ext))
    pending = []
    for n in range(SUBSTEPS):
        last = n == SUBSTEPS - 1
        now = jnp.concatenate([p_own, halo], axis=1)
        if not last:
            q_rim = q_rim - (lap_own[:, RIM] + through(halo, RIM, RIM))
            p_rim = solve(p_rim - q_rim + force_rim, RIM, inv_ref, a_ref, b_ref)
            sends[n] = jnp.transpose(pad_rows(p_rim, LANES))[:hal]
            copies = []
            for k, offset in enumerate(cell_offsets):
                copy = pltpu.make_async_remote_copy(
                    src_ref=sends.at[n, pl.ds(k * slots, slots)],
                    dst_ref=recvs.at[n, pl.ds(k * slots, slots)],
                    send_sem=sends_sem.at[n, k],
                    recv_sem=recvs_sem.at[n, k],
                    device_id=peer(offset),
                    device_id_type=MESH,
                )
                copy.start()
                copies.append(copy)
            pending += copies
        q_own = q_own - (lap_own[:, OWN] + through(halo, RIM, OWN))
        p_own = solve(p_own - q_own + force_own, OWN, inv_ref, a_ref, b_ref)
        if not last:
            sum_one = sum_one + now
            sum_two = sum_two + (SUBSTEPS - n) * now
            lap_own = through(p_own, OWN, slice(0, ext))
            if n == 0:
                trs_ref[...] = pick(tracer_ext, gs_ref[...])
            if n == 1:
                tre_ref[...] = pick(tracer_ext, ge_ref[...])
            if n == SUBSTEPS - 2:
                table = (ge_ref[...].astype(F32) - gs_ref[...].astype(F32)).astype(BF16)
                both = pick(jnp.concatenate([sum_one, sum_two], axis=0), table)
                slope = grad_scale * distance
                flow = velocity - slope * both[:rows]
                gathered = SUBSTEPS * velocity - slope * both[rows:]
                gs_ref[...] = table
            for copy in copies:
                copy.wait_recv()
            halo = jnp.transpose(pad_rows(recvs[n], rim))[:rows]
        else:
            p_out[...] = p_own[:levels]
            change = (grad_scale * distance) * pick(now, gs_ref[...])
            u_out[...] = (flow - change)[:levels, :owned]
            mean = (gathered - change) * (1.0 / SUBSTEPS) * length
            ahead = jnp.maximum(mean, 0.0)
            back = jnp.minimum(mean, 0.0)
            for s in range(species):
                part = slice(s * rows, (s + 1) * rows)
                flux = ahead * trs_ref[part] + back * tre_ref[part]
                change = pick(flux, d_ref[:, OWN]) * (tracer_scale * area)
                t_out[s] = (tracers[s] - change)[:levels]
    for copy in first + efirst + pending:
        copy.wait_send()


def per_device(
    pressure, velocity, tracers, tendency, pattern, coupling, edge_length, inv_distance,
    inv_area, edge_ends, halo_ends, cell_edges, cell_signs, cell_send, edge_send,
):
    stride = max(4, lax.axis_size("blk") // 16)
    cell_offsets = (1, -1, stride, -stride, stride - 1, 1 - stride)
    edge_offsets = (1, stride, -stride, 1 - stride)
    levels, own = pressure.shape
    species = tracers.shape[0]
    owned = velocity.shape[1]
    peers, slots = cell_send.shape
    epeers, eslots = edge_send.shape
    rows = up_to(levels, 8)
    hal = peers * slots
    rim = up_to(hal, LANES)
    ehal = epeers * eslots
    ext, total = own + rim, owned + ehal
    wide = up_to((species + 1) * rows, LANES)
    steps = len(strides(rows))
    sem = pltpu.SemaphoreType.DMA
    vmem = pl.BlockSpec(memory_space=pltpu.VMEM)
    rounds = SUBSTEPS - 1
    return pl.pallas_call(
        functools.partial(kernel, cell_offsets, edge_offsets),
        out_shape=(
            jax.ShapeDtypeStruct(pressure.shape, F32),
            jax.ShapeDtypeStruct(velocity.shape, F32),
            jax.ShapeDtypeStruct(tracers.shape, F32),
        ),
        in_specs=[vmem] * 15,
        out_specs=(vmem, vmem, vmem),
        scratch_shapes=[
            pltpu.VMEM((hal, wide), F32),
            pltpu.VMEM((hal, wide), F32),
            pltpu.VMEM((ehal, LANES), F32),
            pltpu.VMEM((ehal, LANES), F32),
            pltpu.VMEM((rounds, hal, LANES), F32),
            pltpu.VMEM((rounds, hal, LANES), F32),
            pltpu.VMEM((ext, total), BF16),
            pltpu.VMEM((ext, total), BF16),
            pltpu.VMEM((2 * ext, total), BF16),
            pltpu.VMEM((total, ext), BF16),
            pltpu.VMEM((ext, ext), BF16),
            pltpu.VMEM((ext, ext), BF16),
            pltpu.VMEM((steps, rows, ext), F32),
            pltpu.VMEM((steps, rows, ext), F32),
            pltpu.VMEM((rows, ext), F32),
            pltpu.VMEM((species * rows, total), F32),
            pltpu.VMEM((species * rows, total), F32),
            sem((peers,)),
            sem((peers,)),
            sem((epeers,)),
            sem((epeers,)),
            sem((rounds, peers)),
            sem((rounds, peers)),
        ],
        compiler_params=pltpu.CompilerParams(collective_id=0, has_side_effects=True),
    )(
        pressure, velocity, tracers, tendency, pattern.reshape(1, -1), coupling,
        edge_length.reshape(1, -1), inv_distance.reshape(1, -1), inv_area.reshape(1, -1),
        edge_ends, halo_ends, cell_edges, cell_signs, cell_send, edge_send,
    )


def solution(mesh):
    both = ("member", "blk")
    in_specs = (
        P(None, both), P(None, both), P(None, None, both), P(None, both), P(both),
        P(None, "blk"), P("blk"), P("blk"), P("blk"),
        P(None, "blk"), P(None, "blk"), P(None, "blk"), P(None, "blk"), P(None, "blk"),
        P(None, "blk"),
    )
    out_specs = (P(None, both), P(None, both), P(None, None, both))
    return jax.shard_map(
        per_device, mesh=mesh, in_specs=in_specs, out_specs=out_specs, check_vma=False
    )
```

profile of v0, /device:TPU:1, one launch (start us, length us, event | category | flops | bytes accessed | tf_op | source)
XLA Modules:
  0.0 43.3 jit_solution(13845063855672264499)
XLA Ops:
  0.6 0.0 copy-start.1
  0.6 1.3 %reshape.19.len_ref = f32[1,768]{1,0:T(1,128)} reshape(f32[768]{0:T(1024)} %param.21) | data formatting | bytes 6144 | tf_op jit(solution)/shard_map/reshape | solution.py:390
  1.9 0.0 copy-done.1
  1.9 0.6 %reshape.20.dist_ref = f32[1,768]{1,0:T(1,128)} reshape(f32[768]{0:T(1024)S(1)} %copy-done.1) | data formatting | bytes 6144 | tf_op jit(solution)/shard_map/reshape | solution.py:390
  2.5 37.0 %shard_map.166 = (f32[55,256]{1,0:T(8,128)}, f32[55,768]{1,0:T(8,128)}, f32[3,55,256]{2,1,0:T(8,128)}) custom-call(f32[55,256]{1,0:T(8,128)} %p_ref.1, f32[55,768]{1,0:T(8,128)} %u_ref.1, f32[3,55,256]{2,1,0:T(8,128)} %t_ref.1, f32[55,256]{1,0:T(8,128)} %tend_ref.1, f32[1,256]{1,0:T(1,128)} %bitcast.2, f32[55,256]{1,0:T(8,128)} %coup_ref.1, ...), custom_call_target="tpu_custom_call" | custom-call | tf_op jit(solution)/shard_map/pallas_call | solution.py:353
  39.6 1.4 %copy.21 = f32[55,256]{1,0:T(8,128)} copy(f32[55,256]{1,0:T(8,128)} %get-tuple-element.6) | data formatting | bytes 112640
  41.0 0.0 copy-start
  41.0 1.6 %copy.22 = f32[55,768]{1,0:T(8,128)} copy(f32[55,768]{1,0:T(8,128)} %get-tuple-element.7) | data formatting | bytes 337920
  42.6 0.0 copy-done
  42.6 0.7 %copy.23 = f32[3,55,256]{2,1,0:T(8,128)} copy(f32[3,55,256]{2,1,0:T(8,128)S(1)} %copy-done) | data formatting | bytes 337920
Async XLA Ops:
  0.6 1.3 %copy-start.1 = (f32[768]{0:T(1024)S(1)}, f32[768]{0:T(1024)}, u32[]{:S(2)}) copy-start(f32[768]{0:T(1024)} %param.22) | copy-start | bytes 9220
  41.0 1.6 %copy-start = (f32[3,55,256]{2,1,0:T(8,128)S(1)}, f32[3,55,256]{2,1,0:T(8,128)}, u32[]{:S(2)}) copy-start(f32[3,55,256]{2,1,0:T(8,128)} %get-tuple-element.8) | copy-start | bytes 506884
where the time goes:
time: 43.5 us; the launch traced here: 43.3 us
  Pallas kernels  37 us (85%)
  local copies, waits for them, and re-layouts  5.61 us (13%)
  between operations  0.65 us (1%)
    pallas_call x1, Pallas kernels, per_device(): pl.pallas_call(functools.partial(kernel, cell_offsets, edge_offsets), out...  37 us
    unnamed x7, local copies, waits for them, and re-layouts  3.76 us
    reshape x1, local copies, waits for them, and re-layouts, per_device(): edge_length.reshape(1, -1)  1.27 us

commit v1 on v0

--- a/solution.py
+++ b/solution.py
@@ -53,6 +53,19 @@
     return jnp.concatenate(
         [x, jnp.full((x.shape[0], lanes - x.shape[1]), value, x.dtype)], axis=1
     )
+
+
+def row(x):
+    return jnp.concatenate([x[k : k + 1, :] for k in range(x.shape[0])], axis=1)
+
+
+def halo_order(index, own, slots, rim):
+    half = slots // 2
+    shift = half.bit_length() - 1
+    slot = index - own
+    upper = (slot >> shift) & 1
+    moved = ((slot >> (shift + 1)) << shift) + (slot & (half - 1)) + upper * (rim // 2)
+    return jnp.where(index < own, index, own + moved)
 
 
 def one_hot(rows, index):
@@ -85,7 +98,7 @@
     return found
 
 
-def factor_columns(c, levels, inv_ref, a_ref, b_ref):
+def factor_columns(c, levels, lanes, inv_ref, a_ref, b_ref):
     rows = c.shape[0]
     above = up(c, 1, 0.0)
     m = [1.0 + c, c, jnp.ones_like(c), c]
@@ -106,13 +119,13 @@
             m[2] * o[1] + m[3] * o[3],
         ]
     inverse = 1.0 / (above + m[0] / m[2])
-    inv_ref[...] = inverse
-    row = lax.broadcasted_iota(jnp.int32, c.shape, 0)
-    a = jnp.where(row < 1, 0.0, c * inverse)
-    b = jnp.where(row >= levels - 1, 0.0, above * inverse)
+    inv_ref[:, lanes] = inverse
+    height = lax.broadcasted_iota(jnp.int32, c.shape, 0)
+    a = jnp.where(height < 1, 0.0, c * inverse)
+    b = jnp.where(height >= levels - 1, 0.0, above * inverse)
     for number, step in enumerate(strides(rows)):
-        a_ref[number] = a
-        b_ref[number] = b
+        a_ref[number, :, lanes] = a
+        b_ref[number, :, lanes] = b
         a = a * down(a, step, 0.0)
         b = b * up(b, step, 0.0)
 
@@ -129,12 +142,14 @@
 
 def kernel(
     cell_offsets, edge_offsets,
-    p_ref, u_ref, t_ref, tend_ref, pat_ref, coup_ref, len_ref, dist_ref, area_ref,
-    ends_ref, hends_ref, ce_ref, cs_ref, csend_ref, esend_ref,
+    p_hbm, u_hbm, t_hbm, tend_hbm, pat_hbm, coup_hbm, len_hbm, dist_hbm, area_hbm,
+    ends_hbm, hends_hbm, ce_hbm, cs_hbm, csend_hbm, esend_hbm,
     p_out, u_out, t_out,
     send0, recv0, esend, erecv, sends, recvs,
     gs_ref, ge_ref, gc_ref, d_ref, wh_ref, wl_ref, a_ref, b_ref, inv_ref, trs_ref, tre_ref,
-    send0_sem, recv0_sem, esend_sem, erecv_sem, sends_sem, recvs_sem,
+    p_ref, u_ref, t_ref, tend_ref, pat_ref, coup_ref, len_ref, dist_ref, area_ref,
+    ends_ref, hends_ref, ce_ref, cs_ref, csend_ref, esend_ref,
+    load_sem, send0_sem, recv0_sem, esend_sem, erecv_sem, sends_sem, recvs_sem,
 ):
     count = lax.axis_size("blk")
     member = lax.axis_index("member")
@@ -146,6 +161,25 @@
     barrier = pltpu.get_barrier_semaphore()
     for offset in cell_offsets:
         pl.semaphore_signal(barrier, inc=1, device_id=peer(offset), device_id_type=MESH)
+
+    groups = (
+        ((csend_hbm, csend_ref), (p_hbm, p_ref), (t_hbm, t_ref)),
+        ((esend_hbm, esend_ref), (u_hbm, u_ref), (len_hbm, len_ref), (dist_hbm, dist_ref)),
+        ((coup_hbm, coup_ref), (tend_hbm, tend_ref), (pat_hbm, pat_ref), (area_hbm, area_ref)),
+        ((ends_hbm, ends_ref), (hends_hbm, hends_ref), (ce_hbm, ce_ref), (cs_hbm, cs_ref)),
+    )
+    loads = []
+    for group in groups:
+        loads.append([])
+        for source, target in group:
+            number = sum(len(ready) for ready in loads)
+            copy = pltpu.make_async_copy(source, target, load_sem.at[number])
+            copy.start()
+            loads[-1].append(copy)
+
+    def ready(number):
+        for copy in loads[number]:
+            copy.wait()
 
     levels, own = p_ref.shape
     species = t_ref.shape[0]
@@ -159,24 +193,18 @@
     OWN = slice(0, own)
     RIM = slice(own, own + rim)
 
-    csend = jnp.concatenate([csend_ref[k : k + 1, :] for k in range(peers)], axis=1)
+    ready(0)
+    csend = row(csend_ref[...])
     sel = one_hot(own, pad_lanes(csend, rim, -1)).astype(BF16)
-    esel_row = jnp.concatenate([esend_ref[k : k + 1, :] for k in range(epeers)], axis=1)
-    esel = one_hot(owned, esel_row).astype(BF16)
-
     pressure = pad_rows(p_ref[...], rows)
     tracers = [pad_rows(t_ref[s], rows) for s in range(species)]
-    coupling = pad_rows(coup_ref[...], rows)
-    height = lax.broadcasted_iota(jnp.int32, (levels, own), 0).astype(F32)
-    taper = jnp.minimum(1.0, (levels - 1.0 - height) / (0.25 * levels))
-    forcing = pad_rows(force_scale * (1.0 + pat_ref[...] * taper) * tend_ref[...], rows)
-    area = area_ref[...]
-    area8 = pad_rows(area, 8)
     sent = pick(jnp.concatenate([pressure] + tracers, axis=0), sel)
     wide = send0.shape[1]
     send0[...] = jnp.transpose(pad_rows(sent, wide))[:hal]
+    ready(1)
+    esel = one_hot(owned, row(esend_ref[...])).astype(BF16)
     edges = jnp.concatenate(
-        [pad_rows(u_ref[...], rows), len_ref[...], dist_ref[...], jnp.zeros((6, owned), F32)],
+        [pad_rows(u_ref[...], rows), row(len_ref[...]), row(dist_ref[...]), jnp.zeros((6, owned), F32)],
         axis=0,
     )
     esend[...] = jnp.transpose(pad_rows(pick(edges, esel), LANES))
@@ -207,17 +235,24 @@
         copy.start()
         efirst.append(copy)
 
+    ready(2)
+    coupling = pad_rows(coup_ref[...], rows)
+    height = lax.broadcasted_iota(jnp.int32, (levels, own), 0).astype(F32)
+    taper = jnp.minimum(1.0, (levels - 1.0 - height) / (0.25 * levels))
+    forcing = pad_rows(force_scale * (1.0 + row(pat_ref[...]) * taper) * tend_ref[...], rows)
+    area = row(area_ref[...])
+    area8 = pad_rows(area, 8)
     column = jnp.concatenate([coupling, forcing, area8], axis=0)
     column_rim = pick(column, sel)
     force_own, force_rim = forcing, column_rim[rows : 2 * rows]
     area_rim = column_rim[2 * rows : 2 * rows + 1]
-    area_all = jnp.concatenate([area, area_rim], axis=1)
-    factor_columns(
-        jnp.concatenate([coupling, column_rim[:rows]], axis=1), levels, inv_ref, a_ref, b_ref
-    )
-
+    factor_columns(column_rim[:rows], levels, RIM, inv_ref, a_ref, b_ref)
+
+    ready(3)
     start = jnp.concatenate([ends_ref[0:1, :], hends_ref[0:1, :]], axis=1)
     end = jnp.concatenate([ends_ref[1:2, :], hends_ref[1:2, :]], axis=1)
+    start = halo_order(start, own, slots, rim)
+    end = halo_order(end, own, slots, rim)
     ext = own + rim
     gs_ref[...] = one_hot(ext, start).astype(BF16)
     ge_ref[...] = one_hot(ext, end).astype(BF16)
@@ -242,16 +277,31 @@
     gd = ge_ref[...].astype(F32) - gs_ref[...].astype(F32)
     gc_ref[:ext] = (gd * conduct_high).astype(BF16)
     gc_ref[ext:] = (gd * (conduct - conduct_high)).astype(BF16)
-    weight = fold(dot(gc_ref[...], d_ref[...])) * area_all
-    weight_high = weight.astype(BF16)
-    wh_ref[...] = weight_high
-    wl_ref[...] = (weight - weight_high.astype(F32)).astype(BF16)
-    spread = pick(velocity * length, d_ref[...]) * (spread_scale * area_all)
-    q_own, q_rim = spread[:, OWN], spread[:, RIM]
+    flux = velocity * length
+
+    def prepare(lanes, scale):
+        weight = fold(dot(gc_ref[...], d_ref[:, lanes])) * scale
+        weight_high = weight.astype(BF16)
+        wh_ref[:, lanes] = weight_high
+        wl_ref[:, lanes] = (weight - weight_high.astype(F32)).astype(BF16)
+        return pick(flux, d_ref[:, lanes]) * (spread_scale * scale)
+
+    q_rim = prepare(RIM, area_rim)
 
     for copy in first:
         copy.wait_recv()
-    arrived = jnp.transpose(pad_rows(recv0[...], rim))
+    half = slots // 2
+    lower = [recv0[k * slots : k * slots + half] for k in range(peers)]
+    upper = [recv0[k * slots + half : (k + 1) * slots] for k in range(peers)]
+    arrived = jnp.concatenate(
+        [
+            pad_rows(jnp.concatenate(lower, axis=0), rim // 2),
+            pad_rows(jnp.concatenate(upper, axis=0), rim // 2),
+        ],
+        axis=0,
+    )
+    arrived = jnp.transpose(arrived)
+    lane = lax.broadcasted_iota(jnp.int32, (rows, rim), 1)
     halo = arrived[:rows]
     tracer_ext = jnp.concatenate(
         [
@@ -270,20 +320,27 @@
     p_own, p_rim = pressure, sent[:rows]
     sum_one = jnp.zeros((rows, ext), F32)
     sum_two = jnp.zeros((rows, ext), F32)
-    lap_own = through(p_own, OWN, slice(0, ext))
+    lap_rim = through(p_own, OWN, RIM)
     pending = []
     for n in range(SUBSTEPS):
         last = n == SUBSTEPS - 1
         now = jnp.concatenate([p_own, halo], axis=1)
         if not last:
-            q_rim = q_rim - (lap_own[:, RIM] + through(halo, RIM, RIM))
+            q_rim = q_rim - (lap_rim + through(halo, RIM, RIM))
             p_rim = solve(p_rim - q_rim + force_rim, RIM, inv_ref, a_ref, b_ref)
-            sends[n] = jnp.transpose(pad_rows(p_rim, LANES))[:hal]
+            pair = jnp.concatenate(
+                [
+                    pad_rows(p_rim, LANES // 2),
+                    pad_rows(pltpu.roll(p_rim, rim - half, 1), LANES // 2),
+                ],
+                axis=0,
+            )
+            sends[n] = jnp.transpose(pair)[:hal]
             copies = []
             for k, offset in enumerate(cell_offsets):
                 copy = pltpu.make_async_remote_copy(
-                    src_ref=sends.at[n, pl.ds(k * slots, slots)],
-                    dst_ref=recvs.at[n, pl.ds(k * slots, slots)],
+                    src_ref=sends.at[n, pl.ds(k * slots, half)],
+                    dst_ref=recvs.at[n, pl.ds(k * half, half)],
                     send_sem=sends_sem.at[n, k],
                     recv_sem=recvs_sem.at[n, k],
                     device_id=peer(offset),
@@ -292,12 +349,17 @@
                 copy.start()
                 copies.append(copy)
             pending += copies
-        q_own = q_own - (lap_own[:, OWN] + through(halo, RIM, OWN))
+        if n == 0:
+            q_own = prepare(OWN, area)
+            lap_own = through(p_own, OWN, OWN)
+            factor_columns(coupling, levels, OWN, inv_ref, a_ref, b_ref)
+        q_own = q_own - (lap_own + through(halo, RIM, OWN))
         p_own = solve(p_own - q_own + force_own, OWN, inv_ref, a_ref, b_ref)
         if not last:
             sum_one = sum_one + now
             sum_two = sum_two + (SUBSTEPS - n) * now
-            lap_own = through(p_own, OWN, slice(0, ext))
+            lap = through(p_own, OWN, slice(0, ext))
+            lap_own, lap_rim = lap[:, OWN], lap[:, RIM]
             if n == 0:
                 trs_ref[...] = pick(tracer_ext, gs_ref[...])
             if n == 1:
@@ -311,7 +373,9 @@
                 gs_ref[...] = table
             for copy in copies:
                 copy.wait_recv()
-            halo = jnp.transpose(pad_rows(recvs[n], rim))[:rows]
+            both = jnp.transpose(pad_rows(recvs[n], LANES))
+            second = both[LANES // 2 : LANES // 2 + rows]
+            halo = jnp.where(lane < rim // 2, both[:rows], pltpu.roll(second, rim // 2, 1))
         else:
             p_out[...] = p_own[:levels]
             change = (grad_scale * distance) * pick(now, gs_ref[...])
@@ -326,6 +390,17 @@
                 t_out[s] = (tracers[s] - change)[:levels]
     for copy in first + efirst + pending:
         copy.wait_send()
+
+
+def write_out(p_in, u_in, t_in, p_out, u_out, t_out, write_sem):
+    copies = [
+        pltpu.make_async_copy(source, target, write_sem.at[k])
+        for k, (source, target) in enumerate(((t_in, t_out), (u_in, u_out), (p_in, p_out)))
+    ]
+    for copy in copies:
+        copy.start()
+    for copy in copies:
+        copy.wait()
 
 
 def per_device(
@@ -350,14 +425,20 @@
     sem = pltpu.SemaphoreType.DMA
     vmem = pl.BlockSpec(memory_space=pltpu.VMEM)
     rounds = SUBSTEPS - 1
-    return pl.pallas_call(
+    operands = (
+        pressure, velocity, tracers, tendency, pattern.reshape(-1, LANES), coupling,
+        edge_length.reshape(-1, LANES), inv_distance.reshape(-1, LANES),
+        inv_area.reshape(-1, LANES),
+        edge_ends, halo_ends, cell_edges, cell_signs, cell_send, edge_send,
+    )
+    results = pl.pallas_call(
         functools.partial(kernel, cell_offsets, edge_offsets),
         out_shape=(
-            jax.ShapeDtypeStruct(pressure.shape, F32),
-            jax.ShapeDtypeStruct(velocity.shape, F32),
-            jax.ShapeDtypeStruct(tracers.shape, F32),
+            pltpu.VMEM(pressure.shape, F32),
+            pltpu.VMEM(velocity.shape, F32),
+            pltpu.VMEM(tracers.shape, F32),
         ),
-        in_specs=[vmem] * 15,
+        in_specs=[pl.BlockSpec(memory_space=pltpu.HBM)] * 15,
         out_specs=(vmem, vmem, vmem),
         scratch_shapes=[
             pltpu.VMEM((hal, wide), F32),
@@ -365,7 +446,7 @@
             pltpu.VMEM((ehal, LANES), F32),
             pltpu.VMEM((ehal, LANES), F32),
             pltpu.VMEM((rounds, hal, LANES), F32),
-            pltpu.VMEM((rounds, hal, LANES), F32),
+            pltpu.VMEM((rounds, hal // 2, LANES), F32),
             pltpu.VMEM((ext, total), BF16),
             pltpu.VMEM((ext, total), BF16),
             pltpu.VMEM((2 * ext, total), BF16),
@@ -377,6 +458,22 @@
             pltpu.VMEM((rows, ext), F32),
             pltpu.VMEM((species * rows, total), F32),
             pltpu.VMEM((species * rows, total), F32),
+            pltpu.VMEM(pressure.shape, F32),
+            pltpu.VMEM(velocity.shape, F32),
+            pltpu.VMEM(tracers.shape, F32),
+            pltpu.VMEM(tendency.shape, F32),
+            pltpu.VMEM((pattern.shape[0] // LANES, LANES), F32),
+            pltpu.VMEM(coupling.shape, F32),
+            pltpu.VMEM((owned // LANES, LANES), F32),
+            pltpu.VMEM((owned // LANES, LANES), F32),
+            pltpu.VMEM((own // LANES, LANES), F32),
+            pltpu.VMEM(edge_ends.shape, jnp.int32),
+            pltpu.VMEM(halo_ends.shape, jnp.int32),
+            pltpu.VMEM(cell_edges.shape, jnp.int32),
+            pltpu.VMEM(cell_signs.shape, jnp.int32),
+            pltpu.VMEM(cell_send.shape, jnp.int32),
+            pltpu.VMEM(edge_send.shape, jnp.int32),
+            sem((15,)),
             sem((peers,)),
             sem((peers,)),
             sem((epeers,)),
@@ -384,12 +481,19 @@
             sem((rounds, peers)),
             sem((rounds, peers)),
         ],
-        compiler_params=pltpu.CompilerParams(collective_id=0, has_side_effects=True),
-    )(
-        pressure, velocity, tracers, tendency, pattern.reshape(1, -1), coupling,
-        edge_length.reshape(1, -1), inv_distance.reshape(1, -1), inv_area.reshape(1, -1),
-        edge_ends, halo_ends, cell_edges, cell_signs, cell_send, edge_send,
-    )
+        compiler_params=pltpu.CompilerParams(
+            collective_id=0, has_side_effects=True, vmem_limit_bytes=32 * 1024 * 1024
+        ),
+    )(*[pltpu.with_memory_space_constraint(x, pltpu.HBM) for x in operands])
+    anywhere = pl.BlockSpec(memory_space=pl.ANY)
+    return pl.pallas_call(
+        write_out,
+        out_shape=tuple(jax.ShapeDtypeStruct(x.shape, F32) for x in results),
+        in_specs=[vmem] * 3,
+        out_specs=[anywhere] * 3,
+        scratch_shapes=[sem((3,))],
+        compiler_params=pltpu.CompilerParams(vmem_limit_bytes=1024 * 1024),
+    )(*[pltpu.with_memory_space_constraint(x, pltpu.VMEM) for x in results])
 
 
 def solution(mesh):

time: 43.5 us -> 36.2 us (0.83)
  local copies, waits for them, and re-layouts: 5.61 us -> 0 us
  Pallas kernels: 37 us -> 35.4 us
    unnamed x7 -> x0, local copies, waits for them, and re-layouts: 3.76 us -> none
    pallas_call x1, Pallas kernels: 37 us -> 34.6 us  [per_device(): pl.pallas_call(functools.partial(kernel, cell_offsets, edge_offsets), out...]
    reshape x2 -> x0, local copies, waits for them, and re-layouts: 1.85 us -> none  [the longest x1 1.27 us: per_device(): edge_length.reshape(1, -1)]
    pallas_call x0 -> x1, Pallas kernels: none -> 0.76 us  [per_device(): pl.pallas_call(write_out, out_shape=tuple((jax.ShapeDtypeStruct(x.shape,...]
where the time goes in v1:
time: 36.2 us; the launch traced here: 36 us
  Pallas kernels  35.4 us (98%)
  between operations  0.64 us (2%)
    pallas_call x1, Pallas kernels, per_device(): pl.pallas_call(functools.partial(kernel, cell_offsets, edge_offsets), out...  34.6 us
    pallas_call x1, Pallas kernels, per_device(): pl.pallas_call(write_out, out_shape=tuple((jax.ShapeDtypeStruct(x.shape,...  0.76 us

profile of v1, /device:TPU:1, one launch (start us, length us, event | category | flops | bytes accessed | tf_op | source)
XLA Modules:
  0.0 36.0 jit_solution(16388132467605305423)
XLA Ops:
  0.6 34.6 %shard_map.166 = (f32[55,256]{1,0:T(8,128)S(1)}, f32[55,768]{1,0:T(8,128)S(1)}, f32[3,55,256]{2,1,0:T(8,128)S(1)}) custom-call(f32[55,256]{1,0:T(8,128)} %p_hbm.1, f32[55,768]{1,0:T(8,128)} %u_hbm.1, f32[3,55,256]{2,1,0:T(8,128)} %t_hbm.1, f32[55,256]{1,0:T(8,128)} %tend_hbm.1, f32[2,128]{1,0:T(2,128)} %bitcast.6, f32[55,256]{1,0:T(8,128)} %coup_hbm.1, ...), custom_call_target="tpu_custom_call" | custom-call | tf_op jit(solution)/shard_map/pallas_call | solution.py:434
  35.3 0.8 %shard_map.167 = (f32[55,256]{1,0:T(8,128)}, f32[55,768]{1,0:T(8,128)}, f32[3,55,256]{2,1,0:T(8,128)}) custom-call(f32[55,256]{1,0:T(8,128)S(1)} %get-tuple-element.6.p_in, f32[55,768]{1,0:T(8,128)S(1)} %get-tuple-element.7.u_in, f32[3,55,256]{2,1,0:T(8,128)S(1)} %get-tuple-element.8.t_in), custom_call_target="tpu_custom_call" | custom-call | tf_op jit(solution)/shard_map/pallas_call | solution.py:489
